TPU v7x, 32 devices: a whole 2x2x4 slice. The times are simulated.
32 devices in a mesh: gx: 8 (over y, x, core), gz: 4 (over z).
Axes of the slice: x: 2, y: 2, z: 4, core: 2. Of those that a mesh axis runs over, the one named last changes fastest.
Arguments:
- velocity: float32 [3, 64, 64, 512], P(None, 'gx', None, 'gz'), may hold values from -40 to 40
Outputs:
- coefficient: float32 [64], replicated
- eddy_viscosity: float32 [64, 64, 512], P('gx', None, 'gz')
All inputs are finite; a program needn't handle non-finite values.
Results may differ from a plain program's by a relative error of at most 0.0001.
Values sent between devices are 32-bit elements; how exact they have to be, the bound alone decides.
A program may use at most 64 MiB of HBM per device.

v0:
```python
import jax
import jax.numpy as jnp
from jax import lax
from jax.sharding import PartitionSpec as P

index_pairs = ((0, 0), (1, 1), (2, 2), (0, 1), (0, 2), (1, 2))
pair_weights = (1.0, 1.0, 1.0, 2.0, 2.0, 2.0)


def extended(block, sides, width):
    for axis, dim in sides:
        count = lax.axis_size(axis)
        forward = [(i, i + 1) for i in range(count - 1)]
        forward.append((count - 1, 0))
        backward = [(target, source) for source, target in forward]
        low = lax.ppermute(
            lax.slice_in_dim(block, block.shape[dim] - width, None, axis=dim), axis, forward
        )
        high = lax.ppermute(lax.slice_in_dim(block, 0, width, axis=dim), axis, backward)
        block = jnp.concatenate([low, block, high], axis=dim)
    return block


def trim_edges(field):
    return field[..., 1:-1, :, 1:-1]


def along_x(field):
    return 0.5 * (field[..., 2:, :, 1:-1] - field[..., :-2, :, 1:-1])


def along_z(field):
    return 0.5 * (field[..., 1:-1, :, 2:] - field[..., 1:-1, :, :-2])


def along_y(field):
    inside = trim_edges(field)
    middle = 0.5 * (inside[..., 2:, :] - inside[..., :-2, :])
    bottom = inside[..., 1:2, :] - inside[..., 0:1, :]
    upper_end = inside[..., -1:, :] - inside[..., -2:-1, :]
    return jnp.concatenate([bottom, middle, upper_end], axis=-2)


def strain(velocity):
    gradients = [along_x(velocity), along_y(velocity), along_z(velocity)]
    strain_rate = jnp.stack(
        [
            0.5 * (gradients[col_idx][row_idx] + gradients[row_idx][col_idx])
            for row_idx, col_idx in index_pairs
        ]
    )
    weights = jnp.array(pair_weights, dtype=jnp.float32)[:, None, None, None]
    magnitude = jnp.sqrt(2.0 * jnp.sum(weights * strain_rate * strain_rate, axis=0))
    return (strain_rate, magnitude)


def box_filter(field):
    streamwise = 0.25 * (
        field[..., :-2, :, :] + 2.0 * field[..., 1:-1, :, :] + field[..., 2:, :, :]
    )
    return 0.25 * (streamwise[..., :-2] + 2.0 * streamwise[..., 1:-1] + streamwise[..., 2:])


def pair_products(velocity):
    return jnp.stack([velocity[row_idx] * velocity[col_idx] for row_idx, col_idx in index_pairs])


def on_device(velocity):
    wide = extended(velocity, (("gx", 1), ("gz", 3)), 2)
    strain_ext, magnitude_ext = strain(wide)
    filt_prod = box_filter(pair_products(trim_edges(wide)))
    filt_stress = box_filter(magnitude_ext[None] * strain_ext)
    filt_ext = box_filter(wide)
    test_rate, test_mag = strain(filt_ext)
    filt_vel = trim_edges(filt_ext)
    grid_mag = trim_edges(magnitude_ext)
    numer = jnp.zeros((velocity.shape[2],), jnp.float32)
    denom = jnp.zeros((velocity.shape[2],), jnp.float32)
    for slot, (row_idx, col_idx) in enumerate(index_pairs):
        leonard = filt_prod[slot] - filt_vel[row_idx] * filt_vel[col_idx]
        model_term = 2.0 * (filt_stress[slot] - 4.0 * test_mag * test_rate[slot])
        numer = numer + pair_weights[slot] * jnp.sum(leonard * model_term, axis=(0, 2))
        denom = denom + pair_weights[slot] * jnp.sum(model_term * model_term, axis=(0, 2))
    numer, denom = lax.psum((numer, denom), "gx")
    numer, denom = lax.psum((numer, denom), "gz")
    cells = velocity.shape[1] * lax.axis_size("gx") * velocity.shape[3] * lax.axis_size("gz")
    coefficient = numer / cells / (denom / cells + 1e-06)
    eddy_viscosity = coefficient[None, :, None] * grid_mag
    return (coefficient, eddy_viscosity)


def solution(mesh):
    in_specs = (P(None, "gx", None, "gz"),)
    out_specs = (P(), P("gx", None, "gz"))
    return jax.shard_map(
        on_device, mesh=mesh, in_specs=in_specs, out_specs=out_specs, check_vma=False
    )
```

profile of v0, /device:TPU:0, one launch (start us, length us, event | category | flops | bytes accessed | tf_op | source)
XLA Modules:
  0.0 66.7 jit_solution(1675543667405583980)
XLA Ops:
  0.6 1.6 %copy.9 = f32[3,8,64,128]{2,3,1,0:T(8,128)S(1)} copy(f32[3,8,64,128]{3,2,1,0:T(8,128)} %param.3) | data formatting | bytes 1572864 | tf_op args[0]
  2.2 0.1 fusion.75
  2.3 3.4 %collective-permute-start.1 = (f32[3,2,64,128]{2,3,1,0:T(8,128)S(1)}, f32[3,2,64,128]{2,3,1,0:T(8,128)S(1)}, u32[]{:S(2)}, u32[]{:S(2)}) collective-permute-start(f32[3,2,64,128]{2,3,1,0:T(8,128)S(1)} %get-tuple-element.45), channel_id=1, source_target_pairs={{4,0},{8,4},{12,8},{16,12},{20,16},{24,20},{28,24},{0,28},{5,1},{9... | collective-permute-start | bytes 589832 | tf_op jit(solution)/shard_map/ppermute | solution.py:19
  5.7 8.6 %collective-permute-done.1 = f32[3,2,64,128]{2,3,1,0:T(8,128)S(1)} collective-permute-done((f32[3,2,64,128]{2,3,1,0:T(8,128)S(1)}, f32[3,2,64,128]{2,3,1,0:T(8,128)S(1)}, u32[]{:S(2)}, u32[]{:S(2)}) %collective-permute-start.1) | collective-permute-done | bytes 196640 | tf_op jit(solution)/shard_map/ppermute | solution.py:19
  14.3 1.9 %collective-permute-done = f32[3,2,64,128]{2,3,1,0:T(8,128)S(1)} collective-permute-done((f32[3,2,64,128]{2,3,1,0:T(8,128)S(1)}, f32[3,2,64,128]{2,3,1,0:T(8,128)S(1)}, u32[]{:S(2)}, u32[]{:S(2)}) %collective-permute-start) | collective-permute-done | bytes 196640 | tf_op jit(solution)/shard_map/ppermute | solution.py:16
  16.3 3.7 %collective-permute-start.3 = (f32[3,12,64,2]{2,3,1,0:T(2,128)S(1)}, f32[3,12,64,2]{2,3,1,0:T(2,128)S(1)}, u32[]{:S(2)}, u32[]{:S(2)}) collective-permute-start(f32[3,12,64,2]{2,3,1,0:T(2,128)S(1)} %get-tuple-element.39), channel_id=1, source_target_pairs={{1,0},{2,1},{3,2},{0,3},{5,4},{6,5},{7,6},{4,7},{9,8},{10,9},{11,1... | collective-permute-start | bytes 55304 | tf_op jit(solution)/shard_map/ppermute | solution.py:19
  19.9 1.6 %collective-permute-done.3 = f32[3,12,64,2]{2,3,1,0:T(2,128)S(1)} collective-permute-done((f32[3,12,64,2]{2,3,1,0:T(2,128)S(1)}, f32[3,12,64,2]{2,3,1,0:T(2,128)S(1)}, u32[]{:S(2)}, u32[]{:S(2)}) %collective-permute-start.3) | collective-permute-done | bytes 18464 | tf_op jit(solution)/shard_map/ppermute | solution.py:19
  21.6 4.1 %collective-permute-done.2 = f32[3,12,64,2]{2,3,1,0:T(2,128)S(1)} collective-permute-done((f32[3,12,64,2]{2,3,1,0:T(2,128)S(1)}, f32[3,12,64,2]{2,3,1,0:T(2,128)S(1)}, u32[]{:S(2)}, u32[]{:S(2)}) %collective-permute-start.2) | collective-permute-done | bytes 18464 | tf_op jit(solution)/shard_map/ppermute | solution.py:16
  25.7 0.3 pad_maximum_fusion
  26.0 1.7 %slice_subtract_fusion.2 = (f32[3,10,1,130]{2,3,1,0:T(8,128)S(1)}, f32[3,10,1,130]{2,3,1,0:T(8,128)S(1)}) fusion(f32[3,12,64,132]{2,3,1,0:T(8,128)S(1)} %pad_maximum_fusion), kind=kLoop, calls=%fused_computation.32 | loop fusion | flops 7800 | bytes 93600 | tf_op jit(solution)/shard_map/sub | solution.py:39
  27.7 0.6 fusion.12
  28.3 0.3 fusion.16
  28.6 0.5 fusion.14
  29.1 2.4 %slice_subtract_fusion.7 = (f32[3,8,1,128]{2,3,1,0:T(8,128)S(1)}, f32[3,8,1,128]{2,3,1,0:T(8,128)}) fusion(f32[3,10,64,130]{2,3,1,0:T(8,128)S(1)} %fusion.14), kind=kLoop, calls=%fused_computation.50 | loop fusion | flops 6144 | bytes 73728 | tf_op jit(solution)/shard_map/sub | solution.py:39
  31.6 1.6 %fusion.19 = f32[3,8,62,128]{2,3,1,0:T(8,128)} fusion(f32[3,10,64,130]{2,3,1,0:T(8,128)S(1)} %fusion.14), kind=kLoop, calls=%fused_computation.49 | loop fusion | flops 380928 | bytes 2285568 | tf_op jit(solution)/shard_map/mul | solution.py:38
  33.2 0.1 multiply_dynamic-update-slice_fusion.5
  33.3 1.4 %fusion.13 = (f32[3,10,64,130]{2,3,1,0:T(8,128)S(1)}, f32[3,10,64,130]{2,3,1,0:T(8,128)S(1)}) fusion(f32[3,12,64,132]{2,3,1,0:T(8,128)S(1)} %pad_maximum_fusion, f32[3,10,1,130]{2,3,1,0:T(8,128)S(1)} %get-tuple-element.37, f32[3,10,62,130]{2,3,1,0:T(8,128)S(1)} %fusion.12, f32[3,10,1,130]{2,3,1,0:T(8,128)S(1)} %get-tuple-element.36), kind=kLoop, calls=%fused_computation.34 | loop fusion | flops 998400 | bytes 4992000 | tf_op jit(solution)/shard_map/mul | solution.py:29
  34.7 0.1 fusion.30
  34.8 0.4 fusion.11
  35.2 0.1 fusion.26
  35.3 0.1 fusion.24
  35.4 0.1 fusion.22
  35.5 0.5 copy-done.2
  36.0 0.6 fusion
  36.6 0.2 multiply_sqrt_fusion
  36.8 0.3 broadcast_multiply_fusion
  37.2 0.4 fusion.1
  37.6 0.8 %fusion.6 = f32[6,8,64,128]{2,3,1,0:T(8,128)S(1)} fusion(f32[6,8,64,130]{2,3,1,0:T(8,128)S(1)} %fusion.1), kind=kLoop, calls=%fused_computation.13 | loop fusion | flops 1572864 | bytes 6291456 | tf_op jit(solution)/shard_map/mul | solution.py:61
  38.5 0.6 copy-done
  39.0 0.5 copy-done.1
  39.5 1.3 %fusion.18 = (f32[3,8,64,128]{2,3,1,0:T(8,128)S(1)}, f32[3,8,64,128]{2,3,1,0:T(8,128)S(1)}, f32[3,8,64,128]{2,3,1,0:T(8,128)S(1)}) fusion(f32[3,10,64,130]{2,3,1,0:T(8,128)S(1)} %fusion.14, f32[3,8,1,128]{2,3,1,0:T(8,128)S(1)} %copy-done, f32[3,8,62,128]{2,3,1,0:T(8,128)S(1)} %copy-done.1, f32[3,8,1,128]{2,3,1,0:T(8,128)S(1)} %get-tuple-element.42), kind=kLoop, calls=%fused_computation.46 | loop fusion | flops 1179648 | bytes 6291456 | tf_op jit(solution)/shard_map/mul | solution.py:33
  40.9 0.1 fusion.72
  41.0 0.1 fusion.73
  41.1 0.1 fusion.74
  41.1 0.5 fusion.5
  41.6 0.3 multiply_dynamic-update-slice_fusion.4
  41.9 0.1 multiply_dynamic-update-slice_fusion.3
  42.0 0.1 multiply_dynamic-update-slice_fusion.2
  42.1 0.1 multiply_dynamic-update-slice_fusion.1
  42.2 0.1 multiply_dynamic-update-slice_fusion
  42.4 0.4 fusion.3
  42.8 0.8 %fusion.8 = f32[6,8,64,128]{2,3,1,0:T(8,128)S(1)} fusion(f32[6,8,64,130]{2,3,1,0:T(8,128)S(1)} %fusion.3), kind=kLoop, calls=%fused_computation.17 | loop fusion | flops 1572864 | bytes 6291456 | tf_op jit(solution)/shard_map/mul | solution.py:61
  43.6 0.9 %fusion.65 = (f32[8,64,128]{1,2,0:T(8,128)S(1)}, f32[8,64,128]{1,2,0:T(8,128)S(1)}, f32[8,64,128]{1,2,0:T(8,128)S(1)}, f32[8,64,128]{1,2,0:T(8,128)S(1)}, f32[8,...) fusion(f32[6,8,64,128]{2,3,1,0:T(8,128)S(1)} %fusion.6, f32[3,8,64,128]{2,3,1,0:T(8,128)S(1)} %get-tuple-element.41, ...), kind=kLoop, calls=%fused_computation.129 | loop fusion | flops 2097152 | bytes 5767168 | tf_op jit(solution)/shard_map/mul | solution.py:81
  44.5 1.0 %fusion.68 = (f32[64]{0:T(128)S(1)}, f32[64]{0:T(128)S(1)}, f32[64]{0:T(128)S(1)}, f32[64]{0:T(128)S(1)}, f32[64]{0:T(128)S(1)}, /*index=5*/f32[64]{0:T(128)S(1)...) fusion(f32[8,64,128]{1,2,0:T(8,128)S(1)} %get-tuple-element.20,, ...), kind=kLoop, calls=%fused_computation.133 | loop fusion | flops 2358528 | bytes 3935232 | tf_op jit(solution)/shard_map/reduce_sum | solution.py:82
  45.6 11.8 %all-reduce = (f32[64]{0:T(128)S(1)}, f32[64]{0:T(128)S(1)}) all-reduce(f32[64]{0:T(128)S(1)} %multiply_add_fusion, f32[64]{0:T(128)S(1)} %multiply_add_fusion.1), channel_id=1, replica_groups=mesh['gx'=8,'gz'=4] {'gx'}, use_global_device_ids=true, to_apply=%region_16.0 | all-reduce | flops 128 | bytes 1024 | tf_op jit(solution)/shard_map/psum | solution.py:84
  57.4 8.4 %all-reduce.1 = (f32[64]{0:T(128)S(1)}, f32[64]{0:T(128)S(1)}) all-reduce(f32[64]{0:T(128)S(1)} %get-tuple-element.16, f32[64]{0:T(128)S(1)} %get-tuple-element.17), channel_id=1, replica_groups=mesh['gx'=8,'gz'=4] {'gz'}, use_global_device_ids=true, to_apply=%region_17.0 | all-reduce | flops 128 | bytes 1024 | tf_op jit(solution)/shard_map/psum | solution.py:85
  65.8 0.1 slice_multiply_fusion.6
  65.8 0.9 %copy.12 = f32[8,64,128]{2,1,0:T(8,128)} copy(f32[8,64,128]{1,2,0:T(8,128)S(1)} %slice_multiply_fusion.6) | data formatting | bytes 524288
  (16 shorter events, 0.3 us)
Async XLA Ops:
  2.3 12.0 %collective-permute-start.1 = (f32[3,2,64,128]{2,3,1,0:T(8,128)S(1)}, f32[3,2,64,128]{2,3,1,0:T(8,128)S(1)}, u32[]{:S(2)}, u32[]{:S(2)}) collective-permute-start(f32[3,2,64,128]{2,3,1,0:T(8,128)S(1)} %get-tuple-element.45), channel_id=1, source_target_pairs={{4,0},{8,4},{12,8},{16,12},{20,16},{24,20},{28,24},{0,28},{5,1},{9... | collective-permute-start | bytes 589832 | tf_op jit(solution)/shard_map/ppermute | solution.py:19
  5.7 10.5 %collective-permute-start = (f32[3,2,64,128]{2,3,1,0:T(8,128)S(1)}, f32[3,2,64,128]{2,3,1,0:T(8,128)S(1)}, u32[]{:S(2)}, u32[]{:S(2)}) collective-permute-start(f32[3,2,64,128]{2,3,1,0:T(8,128)S(1)} %get-tuple-element.44), channel_id=1, source_target_pairs={{0,4},{4,8},{8,12},{12,16},{16,20},{20,24},{24,28},{28,0},{1,5},{5... | collective-permute-start | bytes 589832 | tf_op jit(solution)/shard_map/ppermute | solution.py:16
  16.3 5.3 %collective-permute-start.3 = (f32[3,12,64,2]{2,3,1,0:T(2,128)S(1)}, f32[3,12,64,2]{2,3,1,0:T(2,128)S(1)}, u32[]{:S(2)}, u32[]{:S(2)}) collective-permute-start(f32[3,12,64,2]{2,3,1,0:T(2,128)S(1)} %get-tuple-element.39), channel_id=1, source_target_pairs={{1,0},{2,1},{3,2},{0,3},{5,4},{6,5},{7,6},{4,7},{9,8},{10,9},{11,1... | collective-permute-start | bytes 55304 | tf_op jit(solution)/shard_map/ppermute | solution.py:19
  19.9 5.8 %collective-permute-start.2 = (f32[3,12,64,2]{2,3,1,0:T(2,128)S(1)}, f32[3,12,64,2]{2,3,1,0:T(2,128)S(1)}, u32[]{:S(2)}, u32[]{:S(2)}) collective-permute-start(f32[3,12,64,2]{2,3,1,0:T(2,128)S(1)} %get-tuple-element.38), channel_id=1, source_target_pairs={{0,1},{1,2},{2,3},{3,0},{4,5},{5,6},{6,7},{7,4},{8,9},{9,10},{10,1... | collective-permute-start | bytes 55304 | tf_op jit(solution)/shard_map/ppermute | solution.py:16
  35.3 0.7 copy-start.2
  37.6 1.4 %copy-start = (f32[3,8,1,128]{2,3,1,0:T(8,128)S(1)}, f32[3,8,1,128]{2,3,1,0:T(8,128)}, u32[]{:S(2)}) copy-start(f32[3,8,1,128]{2,3,1,0:T(8,128)} %get-tuple-element.43) | copy-start | bytes 36868
  37.6 1.9 %copy-start.1 = (f32[3,8,62,128]{2,3,1,0:T(8,128)S(1)}, f32[3,8,62,128]{2,3,1,0:T(8,128)}, u32[]{:S(2)}) copy-start(f32[3,8,62,128]{2,3,1,0:T(8,128)} %fusion.19) | copy-start | bytes 2285572
  65.8 1.0 %copy-start.3 = (f32[64]{0:T(128)}, f32[64]{0:T(128)S(1)}, u32[]{:S(2)}) copy-start(f32[64]{0:T(128)S(1)} %add_divide_fusion) | copy-start | bytes 772
where the time goes:
time: 66.9 us; the launch traced here: 66.7 us
  blocking collectives  20.2 us (30%)
  other arithmetic  18.2 us (27%)
  waiting for transfers between devices  16.3 us (24%)
  starting transfers between devices  7.07 us (11%)
  local copies, waits for them, and re-layouts  4.06 us (6%)
  between operations  0.93 us (1%)
    psum x1, blocking collectives, on_device(): numer, denom = lax.psum((numer, denom), 'gx')  11.8 us
    ppermute x2, waiting for transfers between devices, extended(): lax.ppermute(lax.slice_in_dim(block, 0, width, axis=dim), axis, backward)  10.2 us
    psum x1, blocking collectives, on_device(): numer, denom = lax.psum((numer, denom), 'gz')  8.35 us
    ppermute x2, starting transfers between devices, extended(): lax.ppermute(lax.slice_in_dim(block, 0, width, axis=dim), axis, backward)  7.07 us
    ppermute x2, waiting for transfers between devices, extended(): lax.ppermute(lax.slice_in_dim(block, block.shape[dim] - width, None, axis...  6.04 us
    sub x2, other arithmetic, along_y(): bottom = inside[..., 1:2, :] - inside[..., 0:1, :]  4.1 us
    unnamed x10, local copies, waits for them, and re-layouts  4.01 us
    mul x2, other arithmetic, along_y(): middle = 0.5 * (inside[..., 2:, :] - inside[..., :-2, :])  2.25 us
  transfers between devices with their start and end apart: 4, of which 4 were waited for; matrix products, arithmetic and copies ran while one was open for 0% of the time, Pallas kernels for 0%

commit v1 on v0

v1 whole, which is shorter than its diff:
```python
import functools

import jax
import jax.numpy as jnp
from jax import lax
from jax.experimental import pallas as pl
from jax.experimental.pallas import tpu as pltpu
from jax.sharding import PartitionSpec as P

pairs = ((0, 0), (1, 1), (2, 2), (0, 1), (0, 2), (1, 2))
PAD = 8
MESH = pl.DeviceIdType.MESH


def shear_terms(dx, dy, dz):
    terms = (dx[0], dy[1], dz[2], dx[1] + dy[0], dx[2] + dz[0], dy[2] + dz[1])
    square = [term * term for term in terms]
    total = 0.5 * (square[0] + square[1] + square[2]) + 0.25 * (square[3] + square[4] + square[5])
    return terms, jnp.sqrt(total)


def contraction(leonard, model):
    numer = leonard[0] * model[0]
    for slot in range(1, 6):
        numer = numer + leonard[slot] * model[slot]
    square = [term * term for term in model]
    denom = (square[0] + square[1] + square[2]) + 0.5 * (square[3] + square[4] + square[5])
    return numer, denom


def kernel(
    axes, sizes, cells, vel, coef_out, visc_out,
    U, HU, ST, MAG, ACC, G, RL, RR, row_mine, row_mid, got_x, got_z,
    load_sem, send_sem, recv_sem, sx_send, sx_recv, sz_send, sz_recv,
):
    nx, nz = sizes
    gx, gz = lax.axis_index(axes[0]), lax.axis_index(axes[1])
    X, Y, Z = vel.shape[1:]
    xl, xr = lax.rem(gx + nx - 1, nx), lax.rem(gx + 1, nx)
    zl, zr = lax.rem(gz + nz - 1, nz), lax.rem(gz + 1, nz)
    rows = pl.ds(PAD, Y)

    load = pltpu.make_async_copy(vel, U.at[:, pl.ds(2, X), rows, :], load_sem)
    load.start()

    barrier = pltpu.get_barrier_semaphore()
    peers = [(lax.rem(gx + k, nx), gz) for k in range(1, nx)]
    peers += [(gx, lax.rem(gz + k, nz)) for k in range(1, nz)]
    peers += [(a, b) for a in (xl, xr) for b in (zl, zr)]
    for peer in peers:
        pl.semaphore_signal(barrier, inc=1, device_id=peer, device_id_type=MESH)
    pl.semaphore_wait(barrier, len(peers))

    def send(slot, src, dst, peer):
        copy = pltpu.make_async_remote_copy(
            src_ref=src, dst_ref=dst, send_sem=send_sem.at[slot], recv_sem=recv_sem.at[slot],
            device_id=peer, device_id_type=MESH,
        )
        copy.start()
        return copy

    planes = [
        send(0, vel.at[:, pl.ds(0, 2)], U.at[:, pl.ds(X + 2, 2), rows, :], (xl, gz)),
        send(1, vel.at[:, pl.ds(X - 2, 2)], U.at[:, pl.ds(0, 2), rows, :], (xr, gz)),
    ]
    load.wait()

    lane = lax.broadcasted_iota(jnp.int32, (Y, Z), 1)
    for c in range(3):
        tile = jnp.zeros((Y, Z), jnp.float32)
        for x in range(X):
            rolled = pltpu.roll(U[c, x + 2, PAD:PAD + Y, :], (4 + 8 * x) % Z, 1)
            tile = jnp.where((lane >= 8 * x) & (lane < 8 * x + 8), rolled, tile)
        turned = jnp.concatenate([tile, tile], axis=0).T
        for x in range(X):
            G[c, x + 2] = turned[8 * x:8 * x + 8, :]

    mid, low, high = pl.ds(2, X), pl.ds(2, 2), pl.ds(X, 2)
    before, after = pl.ds(0, 2), pl.ds(X + 2, 2)
    edges = [
        send(2, G.at[:, low], G.at[:, after], (xl, gz)),
        send(3, G.at[:, high], G.at[:, before], (xr, gz)),
        send(4, G.at[:, mid], RL.at[:, mid], (gx, zr)),
        send(5, G.at[:, mid], RR.at[:, mid], (gx, zl)),
        send(6, G.at[:, low], RL.at[:, after], (xl, zr)),
        send(7, G.at[:, high], RL.at[:, before], (xr, zr)),
        send(8, G.at[:, low], RR.at[:, after], (xl, zl)),
        send(9, G.at[:, high], RR.at[:, before], (xr, zl)),
    ]

    def ghosts(ref, first, count):
        span = pl.ds(first, count)
        ref[:, span, PAD - 1:PAD, :] = (
            2.0 * ref[:, span, PAD:PAD + 1, :] - ref[:, span, PAD + 1:PAD + 2, :]
        )
        end = PAD + Y
        ref[:, span, end:end + 1, :] = (
            2.0 * ref[:, span, end - 1:end, :] - ref[:, span, end - 2:end - 1, :]
        )

    def z_sum(f):
        pair = f + pltpu.roll(f, 1, 1)
        return pair + pltpu.roll(pair, Z - 1, 1)

    def z_diff(f):
        return pltpu.roll(f, Z - 1, 1) - pltpu.roll(f, 1, 1)

    def stage_a(p):
        for r in range(PAD, PAD + Y, 8):
            u = [U[i, p, r:r + 8, :] for i in range(3)]
            up = [U[i, p + 1, r:r + 8, :] for i in range(3)]
            um = [U[i, p - 1, r:r + 8, :] for i in range(3)]
            dx = [up[i] - um[i] for i in range(3)]
            dy = [U[i, p, r + 1:r + 9, :] - U[i, p, r - 1:r + 7, :] for i in range(3)]
            dz = [z_diff(u[i]) for i in range(3)]
            terms, mag = shear_terms(dx, dy, dz)
            MAG[p, r - PAD:r - PAD + 8, :] = mag
            for slot in range(6):
                ST[slot, p, r - PAD:r - PAD + 8, :] = mag * terms[slot]
            for i in range(3):
                HU[i, p, r:r + 8, :] = 0.25 * z_sum((up[i] + um[i]) + 2.0 * u[i])
        ghosts(HU, p, 1)

    inner = lax.broadcasted_iota(jnp.int32, (8, Z), 1)
    inner = (inner >= 2) & (inner < Z - 2)

    def stage_b(p):
        for r in range(PAD, PAD + Y, 8):
            q = slice(r - PAD, r - PAD + 8)
            h = [HU[i, p, r:r + 8, :] for i in range(3)]
            dx = [HU[i, p + 1, r:r + 8, :] - HU[i, p - 1, r:r + 8, :] for i in range(3)]
            dy = [HU[i, p, r + 1:r + 9, :] - HU[i, p, r - 1:r + 7, :] for i in range(3)]
            dz = [z_diff(h[i]) for i in range(3)]
            terms, mag = shear_terms(dx, dy, dz)
            mag = 4.0 * mag
            u = [[U[i, p + k, r:r + 8, :] for i in range(3)] for k in (-1, 0, 1)]
            leonard, model = [], []
            for slot, (i, j) in enumerate(pairs):
                prod = (u[0][i] * u[0][j] + u[2][i] * u[2][j]) + 2.0 * (u[1][i] * u[1][j])
                leonard.append(z_sum(prod) - h[i] * h[j])
                stress = (ST[slot, p - 1, q, :] + ST[slot, p + 1, q, :]) + 2.0 * ST[slot, p, q, :]
                model.append(z_sum(stress) - mag * terms[slot])
            numer, denom = contraction(leonard, model)
            ACC[q, :] += jnp.where(inner, numer, 0.0)
            ACC[r - PAD + Y:r - PAD + Y + 8, :] += jnp.where(inner, denom, 0.0)

    def each(first, last, body):
        def step(p, carry):
            body(p)
            return carry

        lax.fori_loop(first, last, step, 0)

    ACC[...] = jnp.zeros_like(ACC)
    ghosts(U, 2, X)
    each(3, X + 1, stage_a)
    each(4, X, stage_b)
    for copy in planes:
        copy.wait_recv()
    ghosts(U, 0, 2)
    ghosts(U, X + 2, 2)
    each(0, 4, lambda s: stage_a(jnp.where(s < 2, s + 1, s + X - 1)))
    each(0, 4, lambda s: stage_b(jnp.where(s < 2, s + 2, s + X - 2)))

    for copy in edges:
        copy.wait_recv()
    W = X + 4
    ln = lax.broadcasted_iota(jnp.int32, (W, 8, 2 * Y), 2)
    sub = lax.broadcasted_iota(jnp.int32, (W, 8, 2 * Y), 1)
    left = ln < Y
    mine = left == (sub >= 4)

    def y_diff(f, n):
        y = ln[:n] - jnp.where(left[:n], 0, Y)
        plus, minus = pltpu.roll(f, 2 * Y - 1, 2), pltpu.roll(f, 1, 2)
        return jnp.where(y == Y - 1, 2.0 * f, jnp.where(y == 0, 2.0 * plus, plus)) - jnp.where(
            y == 0, 2.0 * f, jnp.where(y == Y - 1, 2.0 * minus, minus)
        )

    def s_diff(f):
        return pltpu.roll(f, 7, 1) - pltpu.roll(f, 1, 1)

    def s_sum(f):
        pair = f + pltpu.roll(f, 1, 1)
        return pair + pltpu.roll(pair, 7, 1)

    def x_sum(f):
        return (f[:-2] + f[2:]) + 2.0 * f[1:-1]

    w = [jnp.where(mine, G[c], jnp.where(left, RL[c], RR[c])) for c in range(3)]
    terms, wmag = shear_terms(
        [f[2:] - f[:-2] for f in w],
        [y_diff(f[1:-1], W - 2) for f in w],
        [s_diff(f[1:-1]) for f in w],
    )
    hw = [0.25 * s_sum(x_sum(f)) for f in w]
    test, tmag = shear_terms(
        [f[2:] - f[:-2] for f in hw],
        [y_diff(f[1:-1], X) for f in hw],
        [s_diff(f[1:-1]) for f in hw],
    )
    tmag = 4.0 * tmag
    leonard, model = [], []
    for slot, (i, j) in enumerate(pairs):
        prod = w[i][1:-1] * w[j][1:-1]
        leonard.append(s_sum(x_sum(prod)) - hw[i][1:-1] * hw[j][1:-1])
        model.append(s_sum(x_sum(wmag * terms[slot])) - tmag * test[slot])
    numer, denom = contraction(leonard, model)
    numer, denom = jnp.sum(numer, axis=0), jnp.sum(denom, axis=0)
    s2, l2 = sub[0], left[0]
    take = (l2 & ((s2 == 4) | (s2 == 5))) | (~l2 & ((s2 == 2) | (s2 == 3)))
    numer = jnp.sum(jnp.where(take, numer, 0.0), axis=0, keepdims=True)
    denom = jnp.sum(jnp.where(take, denom, 0.0), axis=0, keepdims=True)
    numer = numer + pltpu.roll(numer, Y, 1)
    denom = denom + pltpu.roll(denom, Y, 1)
    row_mine[...] = jnp.where(l2[:1], numer, denom) + jnp.sum(ACC[...].T, axis=0, keepdims=True)

    def share(mine_ref, got, axis_pos, me, count, ssem, rsem):
        copies = []
        for k in range(1, count):
            other = lax.rem(me + k, count)
            copy = pltpu.make_async_remote_copy(
                src_ref=mine_ref, dst_ref=got.at[k], send_sem=ssem.at[k], recv_sem=rsem.at[k],
                device_id=(other, gz) if axis_pos == 0 else (gx, other), device_id_type=MESH,
            )
            copy.start()
            copies.append(copy)
        return copies

    def gathered(mine_ref, got, copies):
        total = mine_ref[...]
        for k, copy in enumerate(copies):
            copy.wait_recv()
            total = total + got[k + 1]
        return total

    first = share(row_mine, got_x, 0, gx, nx, sx_send, sx_recv)

    back = wmag[1:-1].reshape(8 * X, 2 * Y)
    back = jnp.concatenate([back, jnp.zeros((Z - 8 * X, 2 * Y), jnp.float32)], axis=0).T
    for x in range(X):
        low_lane = pltpu.roll(back[:Y], (Z - 8 * x - 4) % Z, 1)
        high_lane = pltpu.roll(back[Y:], (Z - 1 - 8 * x - 3) % Z, 1)
        mag = MAG[x + 2]
        MAG[x + 2] = jnp.where(lane == 0, low_lane, jnp.where(lane == Z - 1, high_lane, mag))

    row_mid[...] = gathered(row_mine, got_x, first)
    second = share(row_mid, got_z, 1, gz, nz, sz_send, sz_recv)
    total = gathered(row_mid, got_z, second) * (1.0 / (256.0 * cells))
    coef = total / (pltpu.roll(total, Y, 1) + 1e-6)
    coef_out[...] = coef
    wide = jnp.broadcast_to(coef, (Z, 2 * Y)).T[:Y]
    for x in range(X):
        visc_out[x] = wide * MAG[x + 2]
    for copy in planes + edges + first + second:
        copy.wait_send()


def on_device(axes, sizes, velocity):
    X, Y, Z = velocity.shape[1:]
    nx, nz = sizes
    f32 = jnp.float32
    tall = Y + 2 * PAD
    W = X + 4
    dma = pltpu.SemaphoreType.DMA
    cells = X * nx * Z * nz
    coef, visc = pl.pallas_call(
        functools.partial(kernel, axes, sizes, cells),
        out_shape=(
            jax.ShapeDtypeStruct((1, 2 * Y), f32),
            jax.ShapeDtypeStruct((X, Y, Z), f32),
        ),
        in_specs=[pl.BlockSpec(memory_space=pl.ANY)],
        out_specs=(
            pl.BlockSpec(memory_space=pltpu.VMEM),
            pl.BlockSpec(memory_space=pltpu.VMEM),
        ),
        scratch_shapes=[
            pltpu.VMEM((3, W, tall, Z), f32),
            pltpu.VMEM((3, W, tall, Z), f32),
            pltpu.VMEM((6, W, Y, Z), f32),
            pltpu.VMEM((W, Y, Z), f32),
            pltpu.VMEM((2 * Y, Z), f32),
            pltpu.VMEM((3, W, 8, 2 * Y), f32),
            pltpu.VMEM((3, W, 8, 2 * Y), f32),
            pltpu.VMEM((3, W, 8, 2 * Y), f32),
            pltpu.VMEM((1, 2 * Y), f32),
            pltpu.VMEM((1, 2 * Y), f32),
            pltpu.VMEM((nx, 1, 2 * Y), f32),
            pltpu.VMEM((nz, 1, 2 * Y), f32),
            dma,
            dma((10,)),
            dma((10,)),
            dma((nx,)),
            dma((nx,)),
            dma((nz,)),
            dma((nz,)),
        ],
        compiler_params=pltpu.CompilerParams(collective_id=0, has_side_effects=True),
    )(velocity)
    return coef[0, :Y], visc


def solution(mesh):
    axes = ("gx", "gz")
    sizes = tuple(mesh.shape[axis] for axis in axes)
    return jax.shard_map(
        functools.partial(on_device, axes, sizes),
        mesh=mesh,
        in_specs=(P(None, "gx", None, "gz"),),
        out_specs=(P(), P("gx", None, "gz")),
        check_vma=False,
    )
```

time: 66.9 us -> 28.5 us (0.43)
  Pallas kernels: 0 us -> 24.9 us
  blocking collectives: 20.2 us -> 0 us
  other arithmetic: 18.2 us -> 0 us
  waiting for transfers between devices: 16.3 us -> 0 us
  starting transfers between devices: 7.07 us -> 0 us
  local copies, waits for them, and re-layouts: 4.06 us -> 2.75 us
    pallas_call x0 -> x1, Pallas kernels: none -> 24.9 us  [on_device(): pl.pallas_call(functools.partial(kernel, axes, sizes, cells), out_shape=(...]
    psum x2 -> x0, blocking collectives: 20.2 us -> none  [the longest x1 11.8 us: on_device(): numer, denom = lax.psum((numer, denom), 'gx')]
    ppermute x4 -> x0, waiting for transfers between devices: 16.3 us -> none  [the longest x2 10.2 us: extended(): lax.ppermute(lax.slice_in_dim(block, 0, width, axis=dim), axis, backward)]
    mul x14 -> x0, other arithmetic: 9.9 us -> none  [the longest x2 2.25 us: along_y(): middle = 0.5 * (inside[..., 2:, :] - inside[..., :-2, :])]
    ppermute x4 -> x0, starting transfers between devices: 7.07 us -> none  [the longest x2 7.07 us: extended(): lax.ppermute(lax.slice_in_dim(block, 0, width, axis=dim), axis, backward)]
    sub x2 -> x0, other arithmetic: 4.1 us -> none  [along_y(): bottom = inside[..., 1:2, :] - inside[..., 0:1, :]]
    reduce_sum x3 -> x0, other arithmetic: 2.17 us -> none  [the longest x2 1.15 us: strain(): jnp.sum(weights * strain_rate * strain_rate, axis=0)]
    unnamed x10 -> x3, local copies, waits for them, and re-layouts: 4.01 us -> 2.24 us
  transfers between devices with their start and end apart: 4 -> 0, of which waited for: 4 -> 0; matrix products, arithmetic and copies ran while one was open for 0% -> 0% of each run, Pallas kernels for 0% -> 0%
where the time goes in v1:
time: 28.5 us; the launch traced here: 28.3 us
  Pallas kernels  24.9 us (87%)
  local copies, waits for them, and re-layouts  2.75 us (10%)
  between operations  0.65 us (2%)
    pallas_call x1, Pallas kernels, on_device(): pl.pallas_call(functools.partial(kernel, axes, sizes, cells), out_shape=(...  24.9 us
    unnamed x3, local copies, waits for them, and re-layouts  2.24 us

profile of v1, /device:TPU:0, one launch (start us, length us, event | category | flops | bytes accessed | tf_op | source)
XLA Modules:
  0.0 28.3 jit_solution(1661025183711002251)
XLA Ops:
  0.6 24.9 %shard_map.30 = (f32[1,128]{1,0:T(1,128)}, f32[8,64,128]{2,1,0:T(8,128)}) custom-call(f32[3,8,64,128]{3,2,1,0:T(8,128)} %vel.1), custom_call_target="tpu_custom_call" | custom-call | tf_op jit(solution)/shard_map/pallas_call | solution.py:267
  25.5 0.0 copy-start
  25.6 0.6 %copy-done = f32[1,128]{1,0:T(1,128)S(1)} copy-done((f32[1,128]{1,0:T(1,128)S(1)}, f32[1,128]{1,0:T(1,128)}, u32[]{:S(2)}) %copy-start) | copy-done | bytes 536
  26.1 0.5 %slice_bitcast_fusion = f32[64]{0:T(128)} fusion(f32[1,128]{1,0:T(1,128)S(1)} %copy-done), kind=kLoop, calls=%fused_computation | loop fusion | bytes 512 | tf_op jit(solution)/shard_map/squeeze | solution.py:301
  26.6 1.7 %copy.4 = f32[8,64,128]{2,1,0:T(8,128)} copy(f32[8,64,128]{2,1,0:T(8,128)} %get-tuple-element.9) | data formatting | bytes 524288
Async XLA Ops:
  25.5 0.6 %copy-start = (f32[1,128]{1,0:T(1,128)S(1)}, f32[1,128]{1,0:T(1,128)}, u32[]{:S(2)}) copy-start(f32[1,128]{1,0:T(1,128)} %get-tuple-element.4) | copy-start | bytes 1540

commit v2 on v1

--- a/solution.py
+++ b/solution.py
@@ -10,6 +10,7 @@
 pairs = ((0, 0), (1, 1), (2, 2), (0, 1), (0, 2), (1, 2))
 PAD = 8
 MESH = pl.DeviceIdType.MESH
+EARLY_A = True
 
 
 def shear_terms(dx, dy, dz):
@@ -29,27 +30,31 @@
 
 
 def kernel(
-    axes, sizes, cells, vel, coef_out, visc_out,
-    U, HU, ST, MAG, ACC, G, RL, RR, row_mine, row_mid, got_x, got_z,
-    load_sem, send_sem, recv_sem, sx_send, sx_recv, sz_send, sz_recv,
+    axes, sizes, vel, sums_out, mag_out,
+    U, HU, ST, MAG, ACC, LO, HI, RLO, RHI, BACK, GOT,
+    load_sem, send_sem, recv_sem, sum_send, sum_recv,
 ):
     nx, nz = sizes
+    count = nx * nz
     gx, gz = lax.axis_index(axes[0]), lax.axis_index(axes[1])
     X, Y, Z = vel.shape[1:]
     xl, xr = lax.rem(gx + nx - 1, nx), lax.rem(gx + 1, nx)
     zl, zr = lax.rem(gz + nz - 1, nz), lax.rem(gz + 1, nz)
     rows = pl.ds(PAD, Y)
+    me = gx * nz + gz
 
     load = pltpu.make_async_copy(vel, U.at[:, pl.ds(2, X), rows, :], load_sem)
     load.start()
 
+    def to_all(body):
+        def step(k, carry):
+            body((lax.rem(gx + k // nz, nx), lax.rem(gz + lax.rem(k, nz), nz)))
+            return carry
+
+        lax.fori_loop(1, count, step, 0, unroll=min(count - 1, 31))
+
     barrier = pltpu.get_barrier_semaphore()
-    peers = [(lax.rem(gx + k, nx), gz) for k in range(1, nx)]
-    peers += [(gx, lax.rem(gz + k, nz)) for k in range(1, nz)]
-    peers += [(a, b) for a in (xl, xr) for b in (zl, zr)]
-    for peer in peers:
-        pl.semaphore_signal(barrier, inc=1, device_id=peer, device_id_type=MESH)
-    pl.semaphore_wait(barrier, len(peers))
+    to_all(lambda peer: pl.semaphore_signal(barrier, inc=1, device_id=peer, device_id_type=MESH))
 
     def send(slot, src, dst, peer):
         copy = pltpu.make_async_remote_copy(
@@ -59,34 +64,22 @@
         copy.start()
         return copy
 
-    planes = [
-        send(0, vel.at[:, pl.ds(0, 2)], U.at[:, pl.ds(X + 2, 2), rows, :], (xl, gz)),
-        send(1, vel.at[:, pl.ds(X - 2, 2)], U.at[:, pl.ds(0, 2), rows, :], (xr, gz)),
-    ]
     load.wait()
 
     lane = lax.broadcasted_iota(jnp.int32, (Y, Z), 1)
+    span = 4 * X
     for c in range(3):
         tile = jnp.zeros((Y, Z), jnp.float32)
         for x in range(X):
-            rolled = pltpu.roll(U[c, x + 2, PAD:PAD + Y, :], (4 + 8 * x) % Z, 1)
-            tile = jnp.where((lane >= 8 * x) & (lane < 8 * x + 8), rolled, tile)
+            plane = U[c, x + 2, PAD:PAD + Y, :]
+            top = pltpu.roll(plane, (4 + 4 * x) % Z, 1)
+            bottom = pltpu.roll(plane, span + 4 * x, 1)
+            tile = jnp.where((lane >= 4 * x) & (lane < 4 * x + 4), top, tile)
+            tile = jnp.where((lane >= span + 4 * x) & (lane < span + 4 * x + 4), bottom, tile)
         turned = jnp.concatenate([tile, tile], axis=0).T
-        for x in range(X):
-            G[c, x + 2] = turned[8 * x:8 * x + 8, :]
-
-    mid, low, high = pl.ds(2, X), pl.ds(2, 2), pl.ds(X, 2)
-    before, after = pl.ds(0, 2), pl.ds(X + 2, 2)
-    edges = [
-        send(2, G.at[:, low], G.at[:, after], (xl, gz)),
-        send(3, G.at[:, high], G.at[:, before], (xr, gz)),
-        send(4, G.at[:, mid], RL.at[:, mid], (gx, zr)),
-        send(5, G.at[:, mid], RR.at[:, mid], (gx, zl)),
-        send(6, G.at[:, low], RL.at[:, after], (xl, zr)),
-        send(7, G.at[:, high], RL.at[:, before], (xr, zr)),
-        send(8, G.at[:, low], RR.at[:, after], (xl, zl)),
-        send(9, G.at[:, high], RR.at[:, before], (xr, zl)),
-    ]
+        for t in range(X // 2):
+            LO[c, t + 1] = turned[8 * t:8 * t + 8, :]
+            HI[c, t + 1] = turned[span + 8 * t:span + 8 * t + 8, :]
 
     def ghosts(ref, first, count):
         span = pl.ds(first, count)
@@ -153,14 +146,35 @@
 
     ACC[...] = jnp.zeros_like(ACC)
     ghosts(U, 2, X)
-    each(3, X + 1, stage_a)
+    if EARLY_A:
+        each(3, X + 1, stage_a)
+    pl.semaphore_wait(barrier, count - 1)
+
+    half = X // 2
+    mid, low, high = pl.ds(1, half), pl.ds(1, 1), pl.ds(half, 1)
+    before, after = pl.ds(0, 1), pl.ds(half + 1, 1)
+    edges = [
+        send(0, LO.at[:, low], RLO.at[:, after], (xl, zr)),
+        send(1, LO.at[:, high], RLO.at[:, before], (xr, zr)),
+        send(2, HI.at[:, low], RHI.at[:, after], (xl, zl)),
+        send(3, HI.at[:, high], RHI.at[:, before], (xr, zl)),
+        send(4, LO.at[:, mid], RLO.at[:, mid], (gx, zr)),
+        send(5, HI.at[:, mid], RHI.at[:, mid], (gx, zl)),
+        send(6, LO.at[:, low], LO.at[:, after], (xl, gz)),
+        send(7, LO.at[:, high], LO.at[:, before], (xr, gz)),
+        send(8, HI.at[:, low], HI.at[:, after], (xl, gz)),
+        send(9, HI.at[:, high], HI.at[:, before], (xr, gz)),
+    ]
+
+    def send_plane(slot, x, ext, peer):
+        return send(slot, vel.at[:, pl.ds(x, 1)], U.at[:, pl.ds(ext, 1), rows, :], peer)
+
+    near = [send_plane(10, 0, X + 2, (xl, gz)), send_plane(11, X - 1, 1, (xr, gz))]
+    far = [send_plane(12, 1, X + 3, (xl, gz)), send_plane(13, X - 2, 0, (xr, gz))]
+
+    if not EARLY_A:
+        each(3, X + 1, stage_a)
     each(4, X, stage_b)
-    for copy in planes:
-        copy.wait_recv()
-    ghosts(U, 0, 2)
-    ghosts(U, X + 2, 2)
-    each(0, 4, lambda s: stage_a(jnp.where(s < 2, s + 1, s + X - 1)))
-    each(0, 4, lambda s: stage_b(jnp.where(s < 2, s + 2, s + X - 2)))
 
     for copy in edges:
         copy.wait_recv()
@@ -168,7 +182,6 @@
     ln = lax.broadcasted_iota(jnp.int32, (W, 8, 2 * Y), 2)
     sub = lax.broadcasted_iota(jnp.int32, (W, 8, 2 * Y), 1)
     left = ln < Y
-    mine = left == (sub >= 4)
 
     def y_diff(f, n):
         y = ln[:n] - jnp.where(left[:n], 0, Y)
@@ -187,7 +200,16 @@
     def x_sum(f):
         return (f[:-2] + f[2:]) + 2.0 * f[1:-1]
 
-    w = [jnp.where(mine, G[c], jnp.where(left, RL[c], RR[c])) for c in range(3)]
+    w = []
+    head = sub[:2] < 4
+    for c in range(3):
+        found = []
+        for t in range(W // 2):
+            upper = jnp.where(left[0], RLO[c, t], LO[c, t])
+            lower = jnp.where(left[0], HI[c, t], RHI[c, t])
+            found.append(jnp.where(head[0], upper, pltpu.roll(lower, 4, 0)))
+            found.append(jnp.where(head[0], pltpu.roll(upper, 4, 0), lower))
+        w.append(jnp.stack(found))
     terms, wmag = shear_terms(
         [f[2:] - f[:-2] for f in w],
         [y_diff(f[1:-1], W - 2) for f in w],
@@ -213,47 +235,55 @@
     denom = jnp.sum(jnp.where(take, denom, 0.0), axis=0, keepdims=True)
     numer = numer + pltpu.roll(numer, Y, 1)
     denom = denom + pltpu.roll(denom, Y, 1)
-    row_mine[...] = jnp.where(l2[:1], numer, denom) + jnp.sum(ACC[...].T, axis=0, keepdims=True)
-
-    def share(mine_ref, got, axis_pos, me, count, ssem, rsem):
-        copies = []
-        for k in range(1, count):
-            other = lax.rem(me + k, count)
-            copy = pltpu.make_async_remote_copy(
-                src_ref=mine_ref, dst_ref=got.at[k], send_sem=ssem.at[k], recv_sem=rsem.at[k],
-                device_id=(other, gz) if axis_pos == 0 else (gx, other), device_id_type=MESH,
-            )
-            copy.start()
-            copies.append(copy)
-        return copies
-
-    def gathered(mine_ref, got, copies):
-        total = mine_ref[...]
-        for k, copy in enumerate(copies):
-            copy.wait_recv()
-            total = total + got[k + 1]
-        return total
-
-    first = share(row_mine, got_x, 0, gx, nx, sx_send, sx_recv)
+    window_sums = jnp.where(l2[:1], numer, denom)
 
     back = wmag[1:-1].reshape(8 * X, 2 * Y)
     back = jnp.concatenate([back, jnp.zeros((Z - 8 * X, 2 * Y), jnp.float32)], axis=0).T
+    BACK[...] = back
+
+    for copy in near:
+        copy.wait_recv()
+    ghosts(U, 1, 1)
+    ghosts(U, X + 2, 1)
+    each(0, 2, lambda s: stage_a(2 + s * (X - 1)))
+    each(0, 2, lambda s: stage_b(3 + s * (X - 3)))
+    for copy in far:
+        copy.wait_recv()
+    ghosts(U, 0, 1)
+    ghosts(U, X + 3, 1)
+    each(0, 2, lambda s: stage_a(1 + s * (X + 1)))
+    each(0, 2, lambda s: stage_b(2 + s * (X - 1)))
+
+    GOT[me] = window_sums + jnp.sum(ACC[...].T, axis=0, keepdims=True)
+
+    def total_copy(peer):
+        return pltpu.make_async_remote_copy(
+            src_ref=GOT.at[me], dst_ref=GOT.at[me], send_sem=sum_send, recv_sem=sum_recv,
+            device_id=peer, device_id_type=MESH,
+        )
+
+    to_all(lambda peer: total_copy(peer).start())
     for x in range(X):
-        low_lane = pltpu.roll(back[:Y], (Z - 8 * x - 4) % Z, 1)
-        high_lane = pltpu.roll(back[Y:], (Z - 1 - 8 * x - 3) % Z, 1)
+        low_lane = pltpu.roll(BACK[:Y], (Z - 8 * x - 4) % Z, 1)
+        high_lane = pltpu.roll(BACK[Y:], (Z - 1 - 8 * x - 3) % Z, 1)
         mag = MAG[x + 2]
-        MAG[x + 2] = jnp.where(lane == 0, low_lane, jnp.where(lane == Z - 1, high_lane, mag))
-
-    row_mid[...] = gathered(row_mine, got_x, first)
-    second = share(row_mid, got_z, 1, gz, nz, sz_send, sz_recv)
-    total = gathered(row_mid, got_z, second) * (1.0 / (256.0 * cells))
+        mag_out[x] = jnp.where(lane == 0, low_lane, jnp.where(lane == Z - 1, high_lane, mag))
+    for copy in edges + near + far:
+        copy.wait_send()
+    everyone = GOT.at[pl.ds(0, count - 1)]
+    pltpu.make_async_copy(everyone, everyone, sum_recv).wait()
+    sums_out[...] = jnp.sum(GOT[...], axis=0)
+    pltpu.make_async_copy(everyone, everyone, sum_send).wait()
+
+
+def finish(cells, sums, mag, coef_out, visc_out):
+    X, Y, Z = mag.shape
+    total = sums[...] * (1.0 / (256.0 * cells))
     coef = total / (pltpu.roll(total, Y, 1) + 1e-6)
-    coef_out[...] = coef
+    coef_out[...] = coef[0, :Y]
     wide = jnp.broadcast_to(coef, (Z, 2 * Y)).T[:Y]
     for x in range(X):
-        visc_out[x] = wide * MAG[x + 2]
-    for copy in planes + edges + first + second:
-        copy.wait_send()
+        visc_out[x] = wide * mag[x]
 
 
 def on_device(axes, sizes, velocity):
@@ -264,41 +294,42 @@
     W = X + 4
     dma = pltpu.SemaphoreType.DMA
     cells = X * nx * Z * nz
-    coef, visc = pl.pallas_call(
-        functools.partial(kernel, axes, sizes, cells),
+    vmem = pl.BlockSpec(memory_space=pltpu.VMEM)
+    strip = pltpu.VMEM((3, W // 2, 8, 2 * Y), f32)
+    sums, mag = pl.pallas_call(
+        functools.partial(kernel, axes, sizes),
         out_shape=(
             jax.ShapeDtypeStruct((1, 2 * Y), f32),
             jax.ShapeDtypeStruct((X, Y, Z), f32),
         ),
         in_specs=[pl.BlockSpec(memory_space=pl.ANY)],
-        out_specs=(
-            pl.BlockSpec(memory_space=pltpu.VMEM),
-            pl.BlockSpec(memory_space=pltpu.VMEM),
-        ),
+        out_specs=(vmem, vmem),
         scratch_shapes=[
             pltpu.VMEM((3, W, tall, Z), f32),
             pltpu.VMEM((3, W, tall, Z), f32),
             pltpu.VMEM((6, W, Y, Z), f32),
             pltpu.VMEM((W, Y, Z), f32),
             pltpu.VMEM((2 * Y, Z), f32),
-            pltpu.VMEM((3, W, 8, 2 * Y), f32),
-            pltpu.VMEM((3, W, 8, 2 * Y), f32),
-            pltpu.VMEM((3, W, 8, 2 * Y), f32),
-            pltpu.VMEM((1, 2 * Y), f32),
-            pltpu.VMEM((1, 2 * Y), f32),
-            pltpu.VMEM((nx, 1, 2 * Y), f32),
-            pltpu.VMEM((nz, 1, 2 * Y), f32),
+            strip,
+            strip,
+            strip,
+            strip,
+            pltpu.VMEM((2 * Y, Z), f32),
+            pltpu.VMEM((nx * nz, 1, 2 * Y), f32),
             dma,
-            dma((10,)),
-            dma((10,)),
-            dma((nx,)),
-            dma((nx,)),
-            dma((nz,)),
-            dma((nz,)),
+            dma((14,)),
+            dma((14,)),
+            dma,
+            dma,
         ],
         compiler_params=pltpu.CompilerParams(collective_id=0, has_side_effects=True),
     )(velocity)
-    return coef[0, :Y], visc
+    return pl.pallas_call(
+        functools.partial(finish, cells),
+        out_shape=(jax.ShapeDtypeStruct((Y,), f32), jax.ShapeDtypeStruct((X, Y, Z), f32)),
+        in_specs=[vmem, vmem],
+        out_specs=(vmem, vmem),
+    )(sums, mag)
 
 
 def solution(mesh):

time: 28.5 us -> 23.7 us (0.83)
  local copies, waits for them, and re-layouts: 2.75 us -> 0 us
  Pallas kernels: 24.9 us -> 22.9 us
    unnamed x3 -> x0, local copies, waits for them, and re-layouts: 2.24 us -> none
    pallas_call x1 -> x2, Pallas kernels: 24.9 us -> 22.9 us  [the longest x1 21.1 us: on_device(): pl.pallas_call(functools.partial(kernel, axes, sizes), out_shape=(jax.Sha...]
    squeeze x1 -> x0, local copies, waits for them, and re-layouts: 0.51 us -> none  [on_device(): return (coef[0, :Y], visc)]
where the time goes in v2:
time: 23.7 us; the launch traced here: 23.6 us
  Pallas kernels  22.9 us (97%)
  between operations  0.64 us (3%)
    pallas_call x1, Pallas kernels, on_device(): pl.pallas_call(functools.partial(kernel, axes, sizes), out_shape=(jax.Sha...  21.1 us
    pallas_call x1, Pallas kernels, on_device(): pl.pallas_call(functools.partial(finish, cells), out_shape=(jax.ShapeDtyp...  1.82 us

profile of v2, /device:TPU:0, one launch (start us, length us, event | category | flops | bytes accessed | tf_op | source)
XLA Modules:
  0.0 23.6 jit_solution(15905979557076632585)
XLA Ops:
  0.6 21.1 %shard_map.30 = (f32[1,128]{1,0:T(1,128)}, f32[8,64,128]{2,1,0:T(8,128)}) custom-call(f32[3,8,64,128]{3,2,1,0:T(8,128)} %vel.1), custom_call_target="tpu_custom_call" | custom-call | tf_op jit(solution)/shard_map/pallas_call | solution.py:299
  21.7 1.8 %shard_map.31 = (f32[64]{0:T(128)}, f32[8,64,128]{2,1,0:T(8,128)}) custom-call(f32[1,128]{1,0:T(1,128)} %get-tuple-element.4.sums, f32[8,64,128]{2,1,0:T(8,128)} %get-tuple-element.5.mag), custom_call_target="tpu_custom_call" | custom-call | tf_op jit(solution)/shard_map/pallas_call | solution.py:327

commit v3 on v2

--- a/solution.py
+++ b/solution.py
@@ -10,7 +10,7 @@
 pairs = ((0, 0), (1, 1), (2, 2), (0, 1), (0, 2), (1, 2))
 PAD = 8
 MESH = pl.DeviceIdType.MESH
-EARLY_A = True
+EARLY_A = False
 
 
 def shear_terms(dx, dy, dz):
@@ -176,6 +176,12 @@
         each(3, X + 1, stage_a)
     each(4, X, stage_b)
 
+    for copy in near:
+        copy.wait_recv()
+    ghosts(U, 1, 1)
+    ghosts(U, X + 2, 1)
+    each(0, 2, lambda s: stage_a(2 + s * (X - 1)))
+    each(0, 2, lambda s: stage_b(3 + s * (X - 3)))
     for copy in edges:
         copy.wait_recv()
     W = X + 4
@@ -241,12 +247,6 @@
     back = jnp.concatenate([back, jnp.zeros((Z - 8 * X, 2 * Y), jnp.float32)], axis=0).T
     BACK[...] = back
 
-    for copy in near:
-        copy.wait_recv()
-    ghosts(U, 1, 1)
-    ghosts(U, X + 2, 1)
-    each(0, 2, lambda s: stage_a(2 + s * (X - 1)))
-    each(0, 2, lambda s: stage_b(3 + s * (X - 3)))
     for copy in far:
         copy.wait_recv()
     ghosts(U, 0, 1)
@@ -298,10 +298,7 @@
     strip = pltpu.VMEM((3, W // 2, 8, 2 * Y), f32)
     sums, mag = pl.pallas_call(
         functools.partial(kernel, axes, sizes),
-        out_shape=(
-            jax.ShapeDtypeStruct((1, 2 * Y), f32),
-            jax.ShapeDtypeStruct((X, Y, Z), f32),
-        ),
+        out_shape=(pltpu.VMEM((1, 2 * Y), f32), pltpu.VMEM((X, Y, Z), f32)),
         in_specs=[pl.BlockSpec(memory_space=pl.ANY)],
         out_specs=(vmem, vmem),
         scratch_shapes=[
@@ -329,7 +326,7 @@
         out_shape=(jax.ShapeDtypeStruct((Y,), f32), jax.ShapeDtypeStruct((X, Y, Z), f32)),
         in_specs=[vmem, vmem],
         out_specs=(vmem, vmem),
-    )(sums, mag)
+    )(*(pltpu.with_memory_space_constraint(a, pltpu.VMEM) for a in (sums, mag)))
 
 
 def solution(mesh):

time: 23.7 us -> 20.8 us (0.88)
  Pallas kernels: 22.9 us -> 20 us
    pallas_call x1, Pallas kernels: 21.1 us -> 19.1 us  [on_device(): pl.pallas_call(functools.partial(kernel, axes, sizes), out_shape=(pltpu.V...]
    pallas_call x1, Pallas kernels: 1.82 us -> 0.87 us  [on_device(): pl.pallas_call(functools.partial(finish, cells), out_shape=(jax.ShapeDtyp...]
where the time goes in v3:
time: 20.8 us; the launch traced here: 20.6 us
  Pallas kernels  20 us (96%)
  between operations  0.64 us (3%)
    pallas_call x1, Pallas kernels, on_device(): pl.pallas_call(functools.partial(kernel, axes, sizes), out_shape=(pltpu.V...  19.1 us
    pallas_call x1, Pallas kernels, on_device(): pl.pallas_call(functools.partial(finish, cells), out_shape=(jax.ShapeDtyp...  0.87 us

profile of v3, /device:TPU:0, one launch (start us, length us, event | category | flops | bytes accessed | tf_op | source)
XLA Modules:
  0.0 20.6 jit_solution(11395693726139251640)
XLA Ops:
  0.6 19.1 %shard_map.30 = (f32[1,128]{1,0:T(1,128)S(1)}, f32[8,64,128]{2,1,0:T(8,128)S(1)}) custom-call(f32[3,8,64,128]{3,2,1,0:T(8,128)} %vel.1), custom_call_target="tpu_custom_call" | custom-call | tf_op jit(solution)/shard_map/pallas_call | solution.py:299
  19.7 0.9 %shard_map.31 = (f32[64]{0:T(128)}, f32[8,64,128]{2,1,0:T(8,128)}) custom-call(f32[1,128]{1,0:T(1,128)S(1)} %get-tuple-element.4.sums, f32[8,64,128]{2,1,0:T(8,128)S(1)} %get-tuple-element.5.mag), custom_call_target="tpu_custom_call" | custom-call | tf_op jit(solution)/shard_map/pallas_call | solution.py:324
